TPU v7x, 32 devices: a whole 2x2x4 slice. The times are simulated.
32 devices in a mesh: tm: 16 (over z, y, core), asset: 2 (over x).
Axes of the slice: x: 2, y: 2, z: 4, core: 2. Of those that a mesh axis runs over, the one named last changes fastest.
Arguments:
- tick_bars: float32 [2, 16, 61440], P('asset', 'tm'), may hold values from -20 to 20
- prior_bars: float32 [2, 16, 6400], P('asset', 'tm'), may hold values from -20 to 20, as said below
Outputs:
- connectedness: float32 [48, 8192], P('tm', 'asset')
Inputs may be any that keep to these rules, and one draw needn't show every extreme that they name: `prior_bars`: bar returns of the same assets.
All inputs are finite; a program needn't handle non-finite values.
Results may differ from a plain program's by a relative error of at most 0.0014.
Values may be sent and summed in bfloat16 or wider, within the bound.
A program may use at most 64 MiB of HBM per device.

v0:
```python
import math
import jax
import jax.numpy as jnp
from jax import lax
from jax.sharding import PartitionSpec as P

ASSETS = 8192
SPAN = 30
STRIDE = 5
WIN_DEV = 3
LEAD = 25
FLOOR_SQUARES = 1.0


def from_behind(x, axis, by):
    size = lax.axis_size(axis)
    pairs = [(i, i + by) for i in range(size) if 0 <= i + by < size]
    return lax.ppermute(x, axis, pairs)


def swapped(block, axis, distance):
    count = lax.axis_size(axis)
    route = []
    for low in range(count):
        high = low | 1 << distance
        if high != low and high < count:
            route += [(low, high), (high, low)]
    return lax.ppermute(block, axis, route)


def window_stack(extended):
    columns = extended.shape[1]
    groups = extended.reshape(-1, STRIDE, columns)
    stacked = jnp.stack(
        [groups[offset : offset + WIN_DEV] for offset in range(SPAN // STRIDE)], axis=1
    )
    values = stacked.reshape(WIN_DEV, SPAN, columns)
    centred = values - jnp.mean(values, axis=1, keepdims=True)
    squares = jnp.sum(centred * centred, axis=1, keepdims=True)
    return (centred * lax.rsqrt(jnp.maximum(squares, FLOOR_SQUARES))).astype(jnp.bfloat16)


def block_magnitude(left_part, right_part, offset, block_rows):
    correlation = lax.dot_general(
        left_part[:, offset : offset + block_rows],
        right_part,
        (((0,), (0,)), ((), ())),
        preferred_element_type=jnp.float32,
    )
    return jnp.abs(correlation.astype(jnp.bfloat16)).astype(jnp.float32)


def row_totals(own_windows, other_windows):
    columns = own_windows.shape[2]
    block_rows = min(1024, columns)

    def row_one_window(operands):
        left_part, right_part = operands
        pieces = [
            jnp.sum(block_magnitude(left_part, right_part, offset, block_rows), axis=1)
            for offset in range(0, columns, block_rows)
        ]
        return jnp.concatenate(pieces)

    return lax.map(row_one_window, (own_windows, other_windows))


def both_totals(own_windows, other_windows):
    columns = own_windows.shape[2]
    block_rows = min(1024, columns)

    def both_one_window(operands):
        left_part, right_part = operands
        pieces = []
        column_total = jnp.zeros((right_part.shape[1],), jnp.float32)
        for offset in range(0, columns, block_rows):
            magnitude = block_magnitude(left_part, right_part, offset, block_rows)
            pieces.append(jnp.sum(magnitude, axis=1))
            column_total = column_total + jnp.sum(magnitude, axis=0)
        return (jnp.concatenate(pieces), column_total)

    return lax.map(both_one_window, (own_windows, other_windows))


def earlier_rows(tail_rows, distance):
    return from_behind(tail_rows, "tm", distance)


def time_block_rows(tick_bars, prior_bars):
    groups = lax.axis_size("tm")
    group_cols = ASSETS // (2 * groups)
    outgoing = tick_bars.reshape(groups, 1, -1)
    arrived = lax.all_to_all(outgoing, "tm", split_axis=0, concat_axis=1, tiled=True)
    block_len = arrived.shape[2] // group_cols
    own_rows = jnp.transpose(arrived.reshape(groups, block_len, group_cols), (1, 0, 2)).reshape(
        block_len, groups * group_cols
    )
    prior_all = lax.all_gather(prior_bars, "tm", axis=1, tiled=True)
    series_prior = jnp.transpose(prior_all.reshape(groups, LEAD, group_cols), (1, 0, 2)).reshape(
        LEAD, groups * group_cols
    )
    reach = (LEAD + block_len - 1) // block_len
    earlier = []
    for distance in range(reach, 0, -1):
        needed = min(block_len, LEAD - (distance - 1) * block_len)
        earlier.append(earlier_rows(own_rows[block_len - needed :], distance))
    history = jnp.concatenate(earlier, axis=0)
    position = lax.axis_index("tm")
    first_row = position * block_len
    padded = jnp.concatenate([series_prior, jnp.zeros_like(series_prior)], axis=0)
    from_prior = lax.dynamic_slice_in_dim(padded, jnp.minimum(first_row, LEAD), LEAD, 0)
    before_start = first_row - LEAD + jnp.arange(LEAD, dtype=jnp.int32) < 0
    history = jnp.where(before_start[:, None], from_prior, history)
    return jnp.concatenate([history, own_rows], axis=0)


def shards(tick_bars, prior_bars):
    extended = time_block_rows(tick_bars, prior_bars)
    scaled = window_stack(extended)
    columns = scaled.shape[2]
    empty = jnp.zeros((WIN_DEV, columns), jnp.float32)
    partner = swapped(scaled, "asset", 0)
    tile_index = lax.axis_index("asset")
    quarter = columns // 2
    diagonal_part = row_totals(scaled, scaled)
    column_part = empty
    cross_rows = []
    for half_index in range(2):
        mine = scaled[:, :, half_index * quarter : (half_index + 1) * quarter]
        target = (half_index + tile_index) % 2
        theirs = lax.dynamic_slice_in_dim(partner, target * quarter, quarter, 2)
        row_add, column_add = both_totals(mine, theirs)
        cross_rows.append(row_add)
        column_part = lax.dynamic_update_slice_in_dim(column_part, column_add, target * quarter, 1)
    returned = swapped(column_part.astype(jnp.bfloat16), "asset", 0).astype(column_part.dtype)
    totals = diagonal_part + jnp.concatenate(cross_rows, axis=1) + returned
    return totals * (math.sqrt(SPAN) / ASSETS)


def solution(mesh):
    in_specs = (P("asset", "tm", None), P("asset", "tm", None))
    out_specs = P("tm", "asset")
    return jax.shard_map(shards, mesh=mesh, in_specs=in_specs, out_specs=out_specs, check_vma=False)
```

profile of v0, /device:TPU:0, one launch (start us, length us, event | category | flops | bytes accessed | tf_op | source)
XLA Modules:
  0.0 132.5 jit_solution(15997069284028944891)
XLA Ops:
  0.0 7.5 %all-to-all-start = ((f32[16,1,3840]{2,1,0:T(1,128)}), f32[16,1,3840]{2,1,0:T(1,128)S(1)}, u32[]{:S(2)}, u32[]{:S(2)}) async-start(f32[16,1,3840]{2,1,0:T(1,128)} %bitcast.93), calls=%async_computation | async-start | bytes 491520 | tf_op jit(solution)/shard_map/all_to_all | solution.py:93
  7.6 9.8 %all-to-all-done = f32[16,1,3840]{2,1,0:T(1,128)S(1)} async-done(((f32[16,1,3840]{2,1,0:T(1,128)}), f32[16,1,3840]{2,1,0:T(1,128)S(1)}, u32[]{:S(2)}, u32[]{:S(2)}) %all-to-all-start) | async-done | bytes 245792 | tf_op jit(solution)/shard_map/all_to_all | solution.py:93
  17.3 0.6 reduce.9
  18.0 0.1 copy.12
  18.2 0.2 copy.17
  18.3 1.8 %collective-permute-start.1 = (f32[15,4096]{1,0:T(8,128)S(1)}, f32[15,4096]{1,0:T(8,128)S(1)}, u32[]{:S(2)}, u32[]{:S(2)}) collective-permute-start(f32[15,4096]{1,0:T(8,128)S(1)} %bitcast.86), channel_id=1, source_target_pairs={{0,2},{2,4},{4,6},{6,8},{8,10},{10,12},{12,14},{14,16},{16,18},{18... | collective-permute-start | bytes 737288 | tf_op jit(solution)/shard_map/ppermute | solution.py:18
  20.3 0.2 copy.16
  20.4 2.5 %collective-permute-start = (f32[10,4096]{1,0:T(8,128)S(1)}, f32[10,4096]{1,0:T(8,128)S(1)}, u32[]{:S(2)}, u32[]{:S(2)}) collective-permute-start(f32[10,4096]{1,0:T(8,128)S(1)} %bitcast.92), channel_id=1, source_target_pairs={{0,4},{2,6},{4,8},{6,10},{8,12},{10,14},{12,16},{14,18},{16,20},{1... | collective-permute-start | bytes 491528 | tf_op jit(solution)/shard_map/ppermute | solution.py:18
  23.0 22.3 %all_gather.3 = f32[1,16,6400]{2,0,1:T(1,128)S(1)} all-gather(f32[1,1,6400]{2,0,1:T(1,128)S(1)} %bitcast.94), channel_id=1, replica_groups=mesh['tm'=16,'asset'=2] {'tm'}, dimensions={1}, use_global_device_ids=true | all-gather | bytes 435200 | tf_op jit(solution)/shard_map/all_gather | solution.py:98
  45.3 1.0 reduce.8
  46.3 0.2 copy.10
  46.6 0.3 copy.15
  47.1 0.1 fusion.20
  47.2 1.1 pad_maximum_fusion.3
  48.3 0.8 fusion.25
  49.1 1.7 %stack.22 = f32[3,1,5,4096]{3,2,0,1:T(8,128)} reshape(f32[15,4096]{1,0:T(8,128)} %get-tuple-element.124) | data formatting | bytes 491520 | tf_op jit(solution)/shard_map/stack | solution.py:34
  50.8 1.7 %stack.23 = f32[3,1,5,4096]{3,2,0,1:T(8,128)} reshape(f32[15,4096]{1,0:T(8,128)} %get-tuple-element.123) | data formatting | bytes 491520 | tf_op jit(solution)/shard_map/stack | solution.py:34
  52.6 1.0 stack.24
  53.5 1.0 stack.25
  54.5 1.1 fusion.24
  55.7 1.1 fusion.26
  56.8 0.1 fusion.27
  57.0 0.1 fusion.28
  57.1 0.1 fusion.29
  57.3 1.6 %copy.14 = f32[3,6,5,4096]{3,2,1,0:T(8,128)} copy(f32[3,6,5,4096]{3,2,0,1:T(8,128)S(1)} %get-tuple-element.137) | data formatting | bytes 2949120 | tf_op jit(solution)/shard_map/stack | solution.py:34
  59.0 0.4 multiply_reduce_fusion
  59.4 1.7 %reshape.86 = f32[3,30,4096]{2,1,0:T(8,128)S(1)} reshape(f32[3,6,5,4096]{3,2,1,0:T(8,128)} %copy.14) | data formatting | bytes 2949120 | tf_op jit(solution)/shard_map/reshape | solution.py:37
  61.1 0.2 multiply_convert_fusion
  61.3 1.6 %collective-permute-start.2 = (bf16[3,30,4096]{2,1,0:T(8,128)(2,1)S(1)}, bf16[3,30,4096]{2,1,0:T(8,128)(2,1)S(1)}, u32[]{:S(2)}, u32[]{:S(2)}) collective-permute-start(bf16[3,30,4096]{2,1,0:T(8,128)(2,1)S(1)} %multiply_convert_fusion), channel_id=1, source_target_pairs={{0,1},{1,0},{2,3},{3,2},{4,5},{5,4},{6,7},{7,6},{8,9},{9,8},{10,11... | collective-permute-start | bytes 2211848 | tf_op jit(solution)/shard_map/ppermute | solution.py:28
  62.9 18.2 %collective-permute-done.2 = bf16[3,30,4096]{2,1,0:T(8,128)(2,1)S(1)} collective-permute-done((bf16[3,30,4096]{2,1,0:T(8,128)(2,1)S(1)}, bf16[3,30,4096]{2,1,0:T(8,128)(2,1)S(1)}, u32[]{:S(2)}, u32[]{:S(2)}) %collective-permute-start.2) | collective-permute-done | bytes 737312 | tf_op jit(solution)/shard_map/ppermute | solution.py:28
  81.3 9.1 %while.35 = (s32[]{:T(128)}, f32[3,2048]{1,0:T(4,128)S(1)}, f32[3,2048]{1,0:T(4,128)S(1)}, bf16[3,30,2048]{2,1,0:T(8,128)(2,1)S(1)}, bf16[3,30,2048]{2,1,0:T(8,128)(2,1)S(1)}, /*index=5*/s32[]{:T(128)}, s32[]{:T(128)}) while((s32[]{:T(128)}, f32[3,2048]{1,0:T(4,128)S(1)}, f32[3,2048]{1,0:T(4,128)S(1)}, bf16[3,30,2048]{2,1,0:T(8,128)(2,1)S(1)}, ...), condition=%wide.region_18.19_spmd, body=%wide.region_13.18_spmd.sunk | while | flops 272627712 | bytes 737377 | solution.py:82
  81.3 1.4 %convert_reduce_fusion.25 = (f32[2048]{0:T(1024)S(1)}, f32[1024]{0:T(1024)S(1)}) fusion(bf16[3,30,2048]{2,1,0:T(8,128)(2,1)S(1)} %get-tuple-element.289, s32[]{:T(128)} %get-tuple-element.278, bf16[30,2048]{1,0:T(8,128)(2,1)S(1)} %dynamic-slice_bitcast_fusion.7), kind=kOutput, calls=%fused_computation.12.clone.1 | convolution fusion | flops 136311808 | bytes 208900 | tf_op jit(solution)/shard_map/while/body/eval_jaxpr/dot_general | solution.py:44
  82.7 1.4 %convert_reduce_fusion.24 = (f32[2048]{0:T(1024)S(1)}, f32[1024]{0:T(1024)S(1)}) fusion(bf16[3,30,2048]{2,1,0:T(8,128)(2,1)S(1)} %get-tuple-element.289, s32[]{:T(128)} %get-tuple-element.278, bf16[30,2048]{1,0:T(8,128)(2,1)S(1)} %dynamic-slice_bitcast_fusion.7), kind=kOutput, calls=%fused_computation.10.clone.1 | convolution fusion | flops 136311808 | bytes 208900 | tf_op jit(solution)/shard_map/while/body/eval_jaxpr/dot_general | solution.py:44
  84.0 0.1 dynamic_update_slice.34
  84.2 0.1 dynamic_update_slice.33
  84.3 1.4 %convert_reduce_fusion.25 = (f32[2048]{0:T(1024)S(1)}, f32[1024]{0:T(1024)S(1)}) fusion(bf16[3,30,2048]{2,1,0:T(8,128)(2,1)S(1)} %get-tuple-element.289, s32[]{:T(128)} %get-tuple-element.278, bf16[30,2048]{1,0:T(8,128)(2,1)S(1)} %dynamic-slice_bitcast_fusion.7), kind=kOutput, calls=%fused_computation.12.clone.1 | convolution fusion | flops 136311808 | bytes 208900 | tf_op jit(solution)/shard_map/while/body/eval_jaxpr/dot_general | solution.py:44
  85.7 1.4 %convert_reduce_fusion.24 = (f32[2048]{0:T(1024)S(1)}, f32[1024]{0:T(1024)S(1)}) fusion(bf16[3,30,2048]{2,1,0:T(8,128)(2,1)S(1)} %get-tuple-element.289, s32[]{:T(128)} %get-tuple-element.278, bf16[30,2048]{1,0:T(8,128)(2,1)S(1)} %dynamic-slice_bitcast_fusion.7), kind=kOutput, calls=%fused_computation.10.clone.1 | convolution fusion | flops 136311808 | bytes 208900 | tf_op jit(solution)/shard_map/while/body/eval_jaxpr/dot_general | solution.py:44
  87.4 1.4 %convert_reduce_fusion.25 = (f32[2048]{0:T(1024)S(1)}, f32[1024]{0:T(1024)S(1)}) fusion(bf16[3,30,2048]{2,1,0:T(8,128)(2,1)S(1)} %get-tuple-element.289, s32[]{:T(128)} %get-tuple-element.278, bf16[30,2048]{1,0:T(8,128)(2,1)S(1)} %dynamic-slice_bitcast_fusion.7), kind=kOutput, calls=%fused_computation.12.clone.1 | convolution fusion | flops 136311808 | bytes 208900 | tf_op jit(solution)/shard_map/while/body/eval_jaxpr/dot_general | solution.py:44
  88.7 1.4 %convert_reduce_fusion.24 = (f32[2048]{0:T(1024)S(1)}, f32[1024]{0:T(1024)S(1)}) fusion(bf16[3,30,2048]{2,1,0:T(8,128)(2,1)S(1)} %get-tuple-element.289, s32[]{:T(128)} %get-tuple-element.278, bf16[30,2048]{1,0:T(8,128)(2,1)S(1)} %dynamic-slice_bitcast_fusion.7), kind=kOutput, calls=%fused_computation.10.clone.1 | convolution fusion | flops 136311808 | bytes 208900 | tf_op jit(solution)/shard_map/while/body/eval_jaxpr/dot_general | solution.py:44
  90.4 9.2 %while.36 = (s32[]{:T(128)}, f32[3,2048]{1,0:T(4,128)S(1)}, f32[3,2048]{1,0:T(4,128)S(1)}, bf16[3,30,2048]{2,1,0:T(8,128)(2,1)S(1)}, bf16[3,30,2048]{2,1,0:T(8,128)(2,1)S(1)}, /*index=5*/s32[]{:T(128)}, s32[]{:T(128)}) while((s32[]{:T(128)}, f32[3,2048]{1,0:T(4,128)S(1)}, f32[3,2048]{1,0:T(4,128)S(1)}, bf16[3,30,2048]{2,1,0:T(8,128)(2,1)S(1)}, ...), condition=%wide.region_24.25_spmd, body=%wide.region_19.24_spmd.sunk | while | flops 272627712 | bytes 737377 | solution.py:82
  90.5 1.4 %convert_reduce_fusion.27 = (f32[2048]{0:T(1024)S(1)}, f32[1024]{0:T(1024)S(1)}) fusion(bf16[3,30,2048]{2,1,0:T(8,128)(2,1)S(1)} %get-tuple-element.268, s32[]{:T(128)} %get-tuple-element.257, bf16[30,2048]{1,0:T(8,128)(2,1)S(1)} %dynamic-slice_bitcast_fusion.8), kind=kOutput, calls=%fused_computation.28.clone.1 | convolution fusion | flops 136311808 | bytes 208900 | tf_op jit(solution)/shard_map/while/body/eval_jaxpr/dot_general | solution.py:44
  91.8 1.4 %convert_reduce_fusion.26 = (f32[2048]{0:T(1024)S(1)}, f32[1024]{0:T(1024)S(1)}) fusion(bf16[3,30,2048]{2,1,0:T(8,128)(2,1)S(1)} %get-tuple-element.268, s32[]{:T(128)} %get-tuple-element.257, bf16[30,2048]{1,0:T(8,128)(2,1)S(1)} %dynamic-slice_bitcast_fusion.8), kind=kOutput, calls=%fused_computation.26.clone.1 | convolution fusion | flops 136311808 | bytes 208900 | tf_op jit(solution)/shard_map/while/body/eval_jaxpr/dot_general | solution.py:44
  93.5 1.4 %convert_reduce_fusion.27 = (f32[2048]{0:T(1024)S(1)}, f32[1024]{0:T(1024)S(1)}) fusion(bf16[3,30,2048]{2,1,0:T(8,128)(2,1)S(1)} %get-tuple-element.268, s32[]{:T(128)} %get-tuple-element.257, bf16[30,2048]{1,0:T(8,128)(2,1)S(1)} %dynamic-slice_bitcast_fusion.8), kind=kOutput, calls=%fused_computation.28.clone.1 | convolution fusion | flops 136311808 | bytes 208900 | tf_op jit(solution)/shard_map/while/body/eval_jaxpr/dot_general | solution.py:44
  94.9 1.4 %convert_reduce_fusion.26 = (f32[2048]{0:T(1024)S(1)}, f32[1024]{0:T(1024)S(1)}) fusion(bf16[3,30,2048]{2,1,0:T(8,128)(2,1)S(1)} %get-tuple-element.268, s32[]{:T(128)} %get-tuple-element.257, bf16[30,2048]{1,0:T(8,128)(2,1)S(1)} %dynamic-slice_bitcast_fusion.8), kind=kOutput, calls=%fused_computation.26.clone.1 | convolution fusion | flops 136311808 | bytes 208900 | tf_op jit(solution)/shard_map/while/body/eval_jaxpr/dot_general | solution.py:44
  96.6 1.4 %convert_reduce_fusion.27 = (f32[2048]{0:T(1024)S(1)}, f32[1024]{0:T(1024)S(1)}) fusion(bf16[3,30,2048]{2,1,0:T(8,128)(2,1)S(1)} %get-tuple-element.268, s32[]{:T(128)} %get-tuple-element.257, bf16[30,2048]{1,0:T(8,128)(2,1)S(1)} %dynamic-slice_bitcast_fusion.8), kind=kOutput, calls=%fused_computation.28.clone.1 | convolution fusion | flops 136311808 | bytes 208900 | tf_op jit(solution)/shard_map/while/body/eval_jaxpr/dot_general | solution.py:44
  97.9 1.4 %convert_reduce_fusion.26 = (f32[2048]{0:T(1024)S(1)}, f32[1024]{0:T(1024)S(1)}) fusion(bf16[3,30,2048]{2,1,0:T(8,128)(2,1)S(1)} %get-tuple-element.268, s32[]{:T(128)} %get-tuple-element.257, bf16[30,2048]{1,0:T(8,128)(2,1)S(1)} %dynamic-slice_bitcast_fusion.8), kind=kOutput, calls=%fused_computation.26.clone.1 | convolution fusion | flops 136311808 | bytes 208900 | tf_op jit(solution)/shard_map/while/body/eval_jaxpr/dot_general | solution.py:44
  99.7 1.6 %collective-permute-start.3 = (bf16[3,4096]{1,0:T(4,128)(2,1)S(1)}, bf16[3,4096]{1,0:T(4,128)(2,1)S(1)}, u32[]{:S(2)}, u32[]{:S(2)}) collective-permute-start(bf16[3,4096]{1,0:T(4,128)(2,1)S(1)} %convert_element_type.58), channel_id=1, source_target_pairs={{0,1},{1,0},{2,3},{3,2},{4,5},{5,4},{6,7},{7,6},{8,9},{9,8},{10,11... | collective-permute-start | bytes 73736 | tf_op jit(solution)/shard_map/ppermute | solution.py:28
  101.3 30.5 %while.34 = (s32[]{:T(128)}, f32[3,4096]{1,0:T(4,128)S(1)}, bf16[3,30,4096]{2,1,0:T(8,128)(2,1)S(1)}, s32[]{:T(128)}, s32[]{:T(128)}) while((s32[]{:T(128)}, f32[3,4096]{1,0:T(4,128)S(1)}, bf16[3,30,4096]{2,1,0:T(8,128)(2,1)S(1)}, s32[]{:T(128)}, s32[]{:T(128)}) %tuple.68), condition=%wide.region_12.13_spmd, body=%wide.region_7.12_spmd.sunk | while | flops 1073750016 | bytes 1884229 | solution.py:65
  101.5 2.4 %convert_reduce_fusion.20 = f32[1024]{0:T(1024)S(1)} fusion(bf16[30,4096]{1,0:T(8,128)(2,1)S(1)} %dynamic-slice_bitcast_fusion.6), kind=kOutput, calls=%fused_computation.clone.1 | convolution fusion | flops 268434432 | bytes 331776 | tf_op jit(solution)/shard_map/while/body/eval_jaxpr/dot_general | solution.py:44
  104.0 2.5 %convert_reduce_fusion.21 = f32[1024]{0:T(1024)S(1)} fusion(bf16[30,4096]{1,0:T(8,128)(2,1)S(1)} %dynamic-slice_bitcast_fusion.6), kind=kOutput, calls=%fused_computation.1.clone.1 | convolution fusion | flops 268434432 | bytes 331776 | tf_op jit(solution)/shard_map/while/body/eval_jaxpr/dot_general | solution.py:44
  106.4 2.5 %convert_reduce_fusion.22 = f32[1024]{0:T(1024)S(1)} fusion(bf16[30,4096]{1,0:T(8,128)(2,1)S(1)} %dynamic-slice_bitcast_fusion.6), kind=kOutput, calls=%fused_computation.2.clone.1 | convolution fusion | flops 268434432 | bytes 331776 | tf_op jit(solution)/shard_map/while/body/eval_jaxpr/dot_general | solution.py:44
  108.9 2.5 %convert_reduce_fusion.23 = f32[1024]{0:T(1024)S(1)} fusion(bf16[30,4096]{1,0:T(8,128)(2,1)S(1)} %dynamic-slice_bitcast_fusion.6), kind=kOutput, calls=%fused_computation.3.clone.1 | convolution fusion | flops 268434432 | bytes 331776 | tf_op jit(solution)/shard_map/while/body/eval_jaxpr/dot_general | solution.py:44
  111.3 0.2 dynamic_update_slice.32
  111.6 2.4 %convert_reduce_fusion.20 = f32[1024]{0:T(1024)S(1)} fusion(bf16[30,4096]{1,0:T(8,128)(2,1)S(1)} %dynamic-slice_bitcast_fusion.6), kind=kOutput, calls=%fused_computation.clone.1 | convolution fusion | flops 268434432 | bytes 331776 | tf_op jit(solution)/shard_map/while/body/eval_jaxpr/dot_general | solution.py:44
  114.1 2.5 %convert_reduce_fusion.21 = f32[1024]{0:T(1024)S(1)} fusion(bf16[30,4096]{1,0:T(8,128)(2,1)S(1)} %dynamic-slice_bitcast_fusion.6), kind=kOutput, calls=%fused_computation.1.clone.1 | convolution fusion | flops 268434432 | bytes 331776 | tf_op jit(solution)/shard_map/while/body/eval_jaxpr/dot_general | solution.py:44
  116.5 2.5 %convert_reduce_fusion.22 = f32[1024]{0:T(1024)S(1)} fusion(bf16[30,4096]{1,0:T(8,128)(2,1)S(1)} %dynamic-slice_bitcast_fusion.6), kind=kOutput, calls=%fused_computation.2.clone.1 | convolution fusion | flops 268434432 | bytes 331776 | tf_op jit(solution)/shard_map/while/body/eval_jaxpr/dot_general | solution.py:44
  119.0 2.5 %convert_reduce_fusion.23 = f32[1024]{0:T(1024)S(1)} fusion(bf16[30,4096]{1,0:T(8,128)(2,1)S(1)} %dynamic-slice_bitcast_fusion.6), kind=kOutput, calls=%fused_computation.3.clone.1 | convolution fusion | flops 268434432 | bytes 331776 | tf_op jit(solution)/shard_map/while/body/eval_jaxpr/dot_general | solution.py:44
  121.4 0.2 dynamic_update_slice.32
  121.7 2.4 %convert_reduce_fusion.20 = f32[1024]{0:T(1024)S(1)} fusion(bf16[30,4096]{1,0:T(8,128)(2,1)S(1)} %dynamic-slice_bitcast_fusion.6), kind=kOutput, calls=%fused_computation.clone.1 | convolution fusion | flops 268434432 | bytes 331776 | tf_op jit(solution)/shard_map/while/body/eval_jaxpr/dot_general | solution.py:44
  124.2 2.5 %convert_reduce_fusion.21 = f32[1024]{0:T(1024)S(1)} fusion(bf16[30,4096]{1,0:T(8,128)(2,1)S(1)} %dynamic-slice_bitcast_fusion.6), kind=kOutput, calls=%fused_computation.1.clone.1 | convolution fusion | flops 268434432 | bytes 331776 | tf_op jit(solution)/shard_map/while/body/eval_jaxpr/dot_general | solution.py:44
  126.6 2.5 %convert_reduce_fusion.22 = f32[1024]{0:T(1024)S(1)} fusion(bf16[30,4096]{1,0:T(8,128)(2,1)S(1)} %dynamic-slice_bitcast_fusion.6), kind=kOutput, calls=%fused_computation.2.clone.1 | convolution fusion | flops 268434432 | bytes 331776 | tf_op jit(solution)/shard_map/while/body/eval_jaxpr/dot_general | solution.py:44
  129.1 2.5 %convert_reduce_fusion.23 = f32[1024]{0:T(1024)S(1)} fusion(bf16[30,4096]{1,0:T(8,128)(2,1)S(1)} %dynamic-slice_bitcast_fusion.6), kind=kOutput, calls=%fused_computation.3.clone.1 | convolution fusion | flops 268434432 | bytes 331776 | tf_op jit(solution)/shard_map/while/body/eval_jaxpr/dot_general | solution.py:44
  131.6 0.2 dynamic_update_slice.32
  131.8 0.7 fusion.22
  (64 shorter events, 2.3 us)
Async XLA Ops:
  0.0 23.0 %copy-start.1 = (f32[1,1,6400]{2,1,0:T(1,128)S(1)}, f32[1,1,6400]{2,1,0:T(1,128)}, u32[]{:S(2)}) copy-start(f32[1,1,6400]{2,1,0:T(1,128)} %param.9) | copy-start | bytes 76804
  0.0 17.3 %all-to-all-start = ((f32[16,1,3840]{2,1,0:T(1,128)}), f32[16,1,3840]{2,1,0:T(1,128)S(1)}, u32[]{:S(2)}, u32[]{:S(2)}) async-start(f32[16,1,3840]{2,1,0:T(1,128)} %bitcast.93), calls=%async_computation | async-start | bytes 491520 | tf_op jit(solution)/shard_map/all_to_all | solution.py:93
  18.3 28.7 %collective-permute-start.1 = (f32[15,4096]{1,0:T(8,128)S(1)}, f32[15,4096]{1,0:T(8,128)S(1)}, u32[]{:S(2)}, u32[]{:S(2)}) collective-permute-start(f32[15,4096]{1,0:T(8,128)S(1)} %bitcast.86), channel_id=1, source_target_pairs={{0,2},{2,4},{4,6},{6,8},{8,10},{10,12},{12,14},{14,16},{16,18},{18... | collective-permute-start | bytes 737288 | tf_op jit(solution)/shard_map/ppermute | solution.py:18
  20.4 26.6 %collective-permute-start = (f32[10,4096]{1,0:T(8,128)S(1)}, f32[10,4096]{1,0:T(8,128)S(1)}, u32[]{:S(2)}, u32[]{:S(2)}) collective-permute-start(f32[10,4096]{1,0:T(8,128)S(1)} %bitcast.92), channel_id=1, source_target_pairs={{0,4},{2,6},{4,8},{6,10},{8,12},{10,14},{12,16},{14,18},{16,20},{1... | collective-permute-start | bytes 491528 | tf_op jit(solution)/shard_map/ppermute | solution.py:18
  57.3 1.6 %copy-start = (f32[3,4096]{1,0:T(4,128)S(1)}, f32[3,4096]{1,0:T(4,128)}, u32[]{:S(2)}) copy-start(f32[3,4096]{1,0:T(4,128)} %get-tuple-element.128) | copy-start | bytes 147460
  61.3 19.9 %collective-permute-start.2 = (bf16[3,30,4096]{2,1,0:T(8,128)(2,1)S(1)}, bf16[3,30,4096]{2,1,0:T(8,128)(2,1)S(1)}, u32[]{:S(2)}, u32[]{:S(2)}) collective-permute-start(bf16[3,30,4096]{2,1,0:T(8,128)(2,1)S(1)} %multiply_convert_fusion), channel_id=1, source_target_pairs={{0,1},{1,0},{2,3},{3,2},{4,5},{5,4},{6,7},{7,6},{8,9},{9,8},{10,11... | collective-permute-start | bytes 2211848 | tf_op jit(solution)/shard_map/ppermute | solution.py:28
  99.7 32.1 %collective-permute-start.3 = (bf16[3,4096]{1,0:T(4,128)(2,1)S(1)}, bf16[3,4096]{1,0:T(4,128)(2,1)S(1)}, u32[]{:S(2)}, u32[]{:S(2)}) collective-permute-start(bf16[3,4096]{1,0:T(4,128)(2,1)S(1)} %convert_element_type.58), channel_id=1, source_target_pairs={{0,1},{1,0},{2,3},{3,2},{4,5},{5,4},{6,7},{7,6},{8,9},{9,8},{10,11... | collective-permute-start | bytes 73736 | tf_op jit(solution)/shard_map/ppermute | solution.py:28
where the time goes:
time: 133 us; the launch traced here: 132 us
  matrix products  45.7 us (34%)
  waiting for transfers between devices  28 us (21%)
  blocking collectives  22.3 us (17%)
  starting transfers between devices  15 us (11%)
  local copies, waits for them, and re-layouts  12.9 us (10%)
  other arithmetic  7.66 us (6%)
    dot_general x24, matrix products, block_magnitude(): lax.dot_general(left_part[:, offset:offset + block_rows], right_part, (((...  45.7 us
    all_gather x1, blocking collectives, time_block_rows(): prior_all = lax.all_gather(prior_bars, 'tm', axis=1, tiled=True)  22.3 us
    ppermute x2, waiting for transfers between devices, swapped(): return lax.ppermute(block, axis, route)  18.2 us
    all_to_all x1, waiting for transfers between devices, time_block_rows(): lax.all_to_all(outgoing, 'tm', split_axis=0, concat_axis=1, tiled=True)  9.75 us
    all_to_all x1, starting transfers between devices, time_block_rows(): lax.all_to_all(outgoing, 'tm', split_axis=0, concat_axis=1, tiled=True)  7.55 us
    another operation x7, local copies, waits for them, and re-layouts, window_stack(): jnp.stack([groups[offset:offset + WIN_DEV] for offset in range(SPAN // ST...  7.1 us
    ppermute x2, starting transfers between devices, from_behind(): return lax.ppermute(x, axis, pairs)  4.3 us
    reduce_sum x6, other arithmetic, window_stack(): centred = values - jnp.mean(values, axis=1, keepdims=True)  3.52 us
  transfers between devices with their start and end apart: 5, of which 2 were waited for; matrix products, arithmetic and copies ran while one was open for 24% of the time, Pallas kernels for 0%

commit v1 on v0

--- a/solution.py
+++ b/solution.py
@@ -90,7 +90,10 @@
     groups = lax.axis_size("tm")
     group_cols = ASSETS // (2 * groups)
     outgoing = tick_bars.reshape(groups, 1, -1)
-    arrived = lax.all_to_all(outgoing, "tm", split_axis=0, concat_axis=1, tiled=True)
+    arrived = jnp.concatenate(
+        lax.all_to_all(jnp.stack(jnp.split(outgoing, lax.axis_size("tm"), axis=0)), "tm", 0, 0),
+        axis=1,
+    )
     block_len = arrived.shape[2] // group_cols
     own_rows = jnp.transpose(arrived.reshape(groups, block_len, group_cols), (1, 0, 2)).reshape(
         block_len, groups * group_cols

time: 133 us -> 155 us (1.17)
  local copies, waits for them, and re-layouts: 12.9 us -> 33.9 us
    unnamed x10 -> x25, local copies, waits for them, and re-layouts: 0.72 us -> 20.4 us
  transfers between devices with their start and end apart: 5 -> 5, of which waited for: 2 -> 2; matrix products, arithmetic and copies ran while one was open for 24% -> 21% of each run, Pallas kernels for 0% -> 0%
where the time goes in v1:
time: 155 us; the launch traced here: 154 us
  matrix products  45.7 us (29%)
  local copies, waits for them, and re-layouts  33.9 us (22%)
  waiting for transfers between devices  28 us (18%)
  blocking collectives  22.3 us (14%)
  starting transfers between devices  15 us (10%)
  other arithmetic  7.66 us (5%)
    dot_general x24, matrix products, block_magnitude(): lax.dot_general(left_part[:, offset:offset + block_rows], right_part, (((...  45.7 us
    all_gather x1, blocking collectives, time_block_rows(): prior_all = lax.all_gather(prior_bars, 'tm', axis=1, tiled=True)  22.3 us
    unnamed x25, local copies, waits for them, and re-layouts  20.4 us
    ppermute x2, waiting for transfers between devices, swapped(): return lax.ppermute(block, axis, route)  18.2 us
    all_to_all x1, waiting for transfers between devices, time_block_rows(): lax.all_to_all(jnp.stack(jnp.split(outgoing, lax.axis_size('tm'), axis=0)...  9.75 us
    all_to_all x1, starting transfers between devices, time_block_rows(): lax.all_to_all(jnp.stack(jnp.split(outgoing, lax.axis_size('tm'), axis=0)...  7.55 us
    another operation x7, local copies, waits for them, and re-layouts, window_stack(): jnp.stack([groups[offset:offset + WIN_DEV] for offset in range(SPAN // ST...  7.1 us
    ppermute x2, starting transfers between devices, from_behind(): return lax.ppermute(x, axis, pairs)  4.3 us
  transfers between devices with their start and end apart: 5, of which 2 were waited for; matrix products, arithmetic and copies ran while one was open for 21% of the time, Pallas kernels for 0%

profile of v1, /device:TPU:0, one launch (start us, length us, event | category | flops | bytes accessed | tf_op | source)
XLA Modules:
  0.0 153.5 jit_solution(6855125434389436277)
XLA Ops:
  0.0 1.3 constant_dynamic-update-slice_fusion.15
  1.3 1.3 constant_dynamic-update-slice_fusion.14
  2.6 1.3 constant_dynamic-update-slice_fusion.13
  3.9 1.3 constant_dynamic-update-slice_fusion.12
  5.3 1.3 constant_dynamic-update-slice_fusion.11
  6.6 1.3 constant_dynamic-update-slice_fusion.10
  7.9 1.3 constant_dynamic-update-slice_fusion.9
  9.2 1.3 constant_dynamic-update-slice_fusion.8
  10.5 1.3 constant_dynamic-update-slice_fusion.7
  11.8 1.3 constant_dynamic-update-slice_fusion.6
  13.2 1.3 constant_dynamic-update-slice_fusion.5
  14.5 1.3 constant_dynamic-update-slice_fusion.4
  15.8 1.3 constant_dynamic-update-slice_fusion.3
  17.1 1.3 constant_dynamic-update-slice_fusion.2
  18.4 1.3 constant_dynamic-update-slice_fusion.1
  19.7 1.3 constant_dynamic-update-slice_fusion
  21.0 7.5 %all-to-all-start = ((f32[16,1,1,3840]{3,2,1,0:T(1,128)}), f32[16,1,1,3840]{3,2,1,0:T(1,128)S(1)}, u32[]{:S(2)}, u32[]{:S(2)}) async-start(f32[16,1,1,3840]{3,2,1,0:T(1,128)} %constant_dynamic-update-slice_fusion), calls=%async_computation | async-start | bytes 491520 | tf_op jit(solution)/shard_map/all_to_all | solution.py:94
  28.6 9.8 %all-to-all-done = f32[16,1,1,3840]{3,2,1,0:T(1,128)S(1)} async-done(((f32[16,1,1,3840]{3,2,1,0:T(1,128)}), f32[16,1,1,3840]{3,2,1,0:T(1,128)S(1)}, u32[]{:S(2)}, u32[]{:S(2)}) %all-to-all-start) | async-done | bytes 245792 | tf_op jit(solution)/shard_map/all_to_all | solution.py:94
  38.4 0.6 reduce.9
  39.4 1.8 %collective-permute-start.1 = (f32[15,4096]{1,0:T(8,128)S(1)}, f32[15,4096]{1,0:T(8,128)S(1)}, u32[]{:S(2)}, u32[]{:S(2)}) collective-permute-start(f32[15,4096]{1,0:T(8,128)S(1)} %bitcast.117), channel_id=1, source_target_pairs={{0,2},{2,4},{4,6},{6,8},{8,10},{10,12},{12,14},{14,16},{16,18},{18... | collective-permute-start | bytes 737288 | tf_op jit(solution)/shard_map/ppermute | solution.py:18
  41.5 2.5 %collective-permute-start = (f32[10,4096]{1,0:T(8,128)S(1)}, f32[10,4096]{1,0:T(8,128)S(1)}, u32[]{:S(2)}, u32[]{:S(2)}) collective-permute-start(f32[10,4096]{1,0:T(8,128)S(1)} %bitcast.123), channel_id=1, source_target_pairs={{0,4},{2,6},{4,8},{6,10},{8,12},{10,14},{12,16},{14,18},{16,20},{1... | collective-permute-start | bytes 491528 | tf_op jit(solution)/shard_map/ppermute | solution.py:18
  44.0 22.3 %all_gather.3 = f32[1,16,6400]{2,0,1:T(1,128)S(1)} all-gather(f32[1,1,6400]{2,0,1:T(1,128)S(1)} %bitcast.124), channel_id=1, replica_groups=mesh['tm'=16,'asset'=2] {'tm'}, dimensions={1}, use_global_device_ids=true | all-gather | bytes 435200 | tf_op jit(solution)/shard_map/all_gather | solution.py:101
  66.4 1.0 reduce.8
  68.3 1.1 pad_maximum_fusion.3
  69.4 0.8 fusion.25
  70.2 1.7 %stack.90 = f32[3,1,5,4096]{3,2,0,1:T(8,128)} reshape(f32[15,4096]{1,0:T(8,128)} %get-tuple-element.124) | data formatting | bytes 491520 | tf_op jit(solution)/shard_map/stack | solution.py:34
  71.9 1.7 %stack.91 = f32[3,1,5,4096]{3,2,0,1:T(8,128)} reshape(f32[15,4096]{1,0:T(8,128)} %get-tuple-element.123) | data formatting | bytes 491520 | tf_op jit(solution)/shard_map/stack | solution.py:34
  73.6 1.0 stack.92
  74.6 1.0 stack.93
  75.6 1.1 fusion.24
  76.7 1.1 fusion.26
  78.4 1.6 %copy.13 = f32[3,6,5,4096]{3,2,1,0:T(8,128)} copy(f32[3,6,5,4096]{3,2,0,1:T(8,128)S(1)} %get-tuple-element.137) | data formatting | bytes 2949120 | tf_op jit(solution)/shard_map/stack | solution.py:34
  80.4 1.7 %reshape.107 = f32[3,30,4096]{2,1,0:T(8,128)S(1)} reshape(f32[3,6,5,4096]{3,2,1,0:T(8,128)} %copy.13) | data formatting | bytes 2949120 | tf_op jit(solution)/shard_map/reshape | solution.py:37
  82.3 1.6 %collective-permute-start.2 = (bf16[3,30,4096]{2,1,0:T(8,128)(2,1)S(1)}, bf16[3,30,4096]{2,1,0:T(8,128)(2,1)S(1)}, u32[]{:S(2)}, u32[]{:S(2)}) collective-permute-start(bf16[3,30,4096]{2,1,0:T(8,128)(2,1)S(1)} %multiply_convert_fusion), channel_id=1, source_target_pairs={{0,1},{1,0},{2,3},{3,2},{4,5},{5,4},{6,7},{7,6},{8,9},{9,8},{10,11... | collective-permute-start | bytes 2211848 | tf_op jit(solution)/shard_map/ppermute | solution.py:28
  84.0 18.2 %collective-permute-done.2 = bf16[3,30,4096]{2,1,0:T(8,128)(2,1)S(1)} collective-permute-done((bf16[3,30,4096]{2,1,0:T(8,128)(2,1)S(1)}, bf16[3,30,4096]{2,1,0:T(8,128)(2,1)S(1)}, u32[]{:S(2)}, u32[]{:S(2)}) %collective-permute-start.2) | collective-permute-done | bytes 737312 | tf_op jit(solution)/shard_map/ppermute | solution.py:28
  102.3 9.1 %while.35 = (s32[]{:T(128)}, f32[3,2048]{1,0:T(4,128)S(1)}, f32[3,2048]{1,0:T(4,128)S(1)}, bf16[3,30,2048]{2,1,0:T(8,128)(2,1)S(1)}, bf16[3,30,2048]{2,1,0:T(8,128)(2,1)S(1)}, /*index=5*/s32[]{:T(128)}, s32[]{:T(128)}) while((s32[]{:T(128)}, f32[3,2048]{1,0:T(4,128)S(1)}, f32[3,2048]{1,0:T(4,128)S(1)}, bf16[3,30,2048]{2,1,0:T(8,128)(2,1)S(1)}, ...), condition=%wide.region_18.19_spmd, body=%wide.region_13.18_spmd.sunk | while | flops 272627712 | bytes 737377 | solution.py:82
  102.3 1.4 convert_reduce_fusion.25
  103.7 1.4 convert_reduce_fusion.24
  105.4 1.4 convert_reduce_fusion.25
  106.7 1.4 convert_reduce_fusion.24
  108.4 1.4 convert_reduce_fusion.25
  109.8 1.4 convert_reduce_fusion.24
  111.5 9.2 %while.36 = (s32[]{:T(128)}, f32[3,2048]{1,0:T(4,128)S(1)}, f32[3,2048]{1,0:T(4,128)S(1)}, bf16[3,30,2048]{2,1,0:T(8,128)(2,1)S(1)}, bf16[3,30,2048]{2,1,0:T(8,128)(2,1)S(1)}, /*index=5*/s32[]{:T(128)}, s32[]{:T(128)}) while((s32[]{:T(128)}, f32[3,2048]{1,0:T(4,128)S(1)}, f32[3,2048]{1,0:T(4,128)S(1)}, bf16[3,30,2048]{2,1,0:T(8,128)(2,1)S(1)}, ...), condition=%wide.region_24.25_spmd, body=%wide.region_19.24_spmd.sunk | while | flops 272627712 | bytes 737377 | solution.py:82
  111.5 1.4 convert_reduce_fusion.27
  112.9 1.4 convert_reduce_fusion.26
  114.6 1.4 convert_reduce_fusion.27
  115.9 1.4 convert_reduce_fusion.26
  117.6 1.4 convert_reduce_fusion.27
  119.0 1.4 convert_reduce_fusion.26
  120.7 1.6 %collective-permute-start.3 = (bf16[3,4096]{1,0:T(4,128)(2,1)S(1)}, bf16[3,4096]{1,0:T(4,128)(2,1)S(1)}, u32[]{:S(2)}, u32[]{:S(2)}) collective-permute-start(bf16[3,4096]{1,0:T(4,128)(2,1)S(1)} %convert_element_type.58), channel_id=1, source_target_pairs={{0,1},{1,0},{2,3},{3,2},{4,5},{5,4},{6,7},{7,6},{8,9},{9,8},{10,11... | collective-permute-start | bytes 73736 | tf_op jit(solution)/shard_map/ppermute | solution.py:28
  122.3 30.5 %while.34 = (s32[]{:T(128)}, f32[3,4096]{1,0:T(4,128)S(1)}, bf16[3,30,4096]{2,1,0:T(8,128)(2,1)S(1)}, s32[]{:T(128)}, s32[]{:T(128)}) while((s32[]{:T(128)}, f32[3,4096]{1,0:T(4,128)S(1)}, bf16[3,30,4096]{2,1,0:T(8,128)(2,1)S(1)}, s32[]{:T(128)}, s32[]{:T(128)}) %tuple.68), condition=%wide.region_12.13_spmd, body=%wide.region_7.12_spmd.sunk | while | flops 1073750016 | bytes 1884229 | solution.py:65
  122.6 2.4 %convert_reduce_fusion.20 = f32[1024]{0:T(1024)S(1)} fusion(bf16[30,4096]{1,0:T(8,128)(2,1)S(1)} %dynamic-slice_bitcast_fusion.6), kind=kOutput, calls=%fused_computation.clone.1 | convolution fusion | flops 268434432 | bytes 331776 | tf_op jit(solution)/shard_map/while/body/eval_jaxpr/dot_general | solution.py:44
  125.0 2.5 %convert_reduce_fusion.21 = f32[1024]{0:T(1024)S(1)} fusion(bf16[30,4096]{1,0:T(8,128)(2,1)S(1)} %dynamic-slice_bitcast_fusion.6), kind=kOutput, calls=%fused_computation.1.clone.1 | convolution fusion | flops 268434432 | bytes 331776 | tf_op jit(solution)/shard_map/while/body/eval_jaxpr/dot_general | solution.py:44
  127.5 2.5 %convert_reduce_fusion.22 = f32[1024]{0:T(1024)S(1)} fusion(bf16[30,4096]{1,0:T(8,128)(2,1)S(1)} %dynamic-slice_bitcast_fusion.6), kind=kOutput, calls=%fused_computation.2.clone.1 | convolution fusion | flops 268434432 | bytes 331776 | tf_op jit(solution)/shard_map/while/body/eval_jaxpr/dot_general | solution.py:44
  129.9 2.5 %convert_reduce_fusion.23 = f32[1024]{0:T(1024)S(1)} fusion(bf16[30,4096]{1,0:T(8,128)(2,1)S(1)} %dynamic-slice_bitcast_fusion.6), kind=kOutput, calls=%fused_computation.3.clone.1 | convolution fusion | flops 268434432 | bytes 331776 | tf_op jit(solution)/shard_map/while/body/eval_jaxpr/dot_general | solution.py:44
  132.7 2.4 %convert_reduce_fusion.20 = f32[1024]{0:T(1024)S(1)} fusion(bf16[30,4096]{1,0:T(8,128)(2,1)S(1)} %dynamic-slice_bitcast_fusion.6), kind=kOutput, calls=%fused_computation.clone.1 | convolution fusion | flops 268434432 | bytes 331776 | tf_op jit(solution)/shard_map/while/body/eval_jaxpr/dot_general | solution.py:44
  135.1 2.5 %convert_reduce_fusion.21 = f32[1024]{0:T(1024)S(1)} fusion(bf16[30,4096]{1,0:T(8,128)(2,1)S(1)} %dynamic-slice_bitcast_fusion.6), kind=kOutput, calls=%fused_computation.1.clone.1 | convolution fusion | flops 268434432 | bytes 331776 | tf_op jit(solution)/shard_map/while/body/eval_jaxpr/dot_general | solution.py:44
  137.6 2.5 %convert_reduce_fusion.22 = f32[1024]{0:T(1024)S(1)} fusion(bf16[30,4096]{1,0:T(8,128)(2,1)S(1)} %dynamic-slice_bitcast_fusion.6), kind=kOutput, calls=%fused_computation.2.clone.1 | convolution fusion | flops 268434432 | bytes 331776 | tf_op jit(solution)/shard_map/while/body/eval_jaxpr/dot_general | solution.py:44
  140.0 2.5 %convert_reduce_fusion.23 = f32[1024]{0:T(1024)S(1)} fusion(bf16[30,4096]{1,0:T(8,128)(2,1)S(1)} %dynamic-slice_bitcast_fusion.6), kind=kOutput, calls=%fused_computation.3.clone.1 | convolution fusion | flops 268434432 | bytes 331776 | tf_op jit(solution)/shard_map/while/body/eval_jaxpr/dot_general | solution.py:44
  142.8 2.4 %convert_reduce_fusion.20 = f32[1024]{0:T(1024)S(1)} fusion(bf16[30,4096]{1,0:T(8,128)(2,1)S(1)} %dynamic-slice_bitcast_fusion.6), kind=kOutput, calls=%fused_computation.clone.1 | convolution fusion | flops 268434432 | bytes 331776 | tf_op jit(solution)/shard_map/while/body/eval_jaxpr/dot_general | solution.py:44
  145.2 2.5 %convert_reduce_fusion.21 = f32[1024]{0:T(1024)S(1)} fusion(bf16[30,4096]{1,0:T(8,128)(2,1)S(1)} %dynamic-slice_bitcast_fusion.6), kind=kOutput, calls=%fused_computation.1.clone.1 | convolution fusion | flops 268434432 | bytes 331776 | tf_op jit(solution)/shard_map/while/body/eval_jaxpr/dot_general | solution.py:44
  147.7 2.5 %convert_reduce_fusion.22 = f32[1024]{0:T(1024)S(1)} fusion(bf16[30,4096]{1,0:T(8,128)(2,1)S(1)} %dynamic-slice_bitcast_fusion.6), kind=kOutput, calls=%fused_computation.2.clone.1 | convolution fusion | flops 268434432 | bytes 331776 | tf_op jit(solution)/shard_map/while/body/eval_jaxpr/dot_general | solution.py:44
  150.1 2.5 %convert_reduce_fusion.23 = f32[1024]{0:T(1024)S(1)} fusion(bf16[30,4096]{1,0:T(8,128)(2,1)S(1)} %dynamic-slice_bitcast_fusion.6), kind=kOutput, calls=%fused_computation.3.clone.1 | convolution fusion | flops 268434432 | bytes 331776 | tf_op jit(solution)/shard_map/while/body/eval_jaxpr/dot_general | solution.py:44
  152.9 0.7 fusion.22
  (80 shorter events, 5.5 us)
Async XLA Ops:
  21.0 23.0 %copy-start.1 = (f32[1,1,6400]{2,1,0:T(1,128)S(1)}, f32[1,1,6400]{2,1,0:T(1,128)}, u32[]{:S(2)}) copy-start(f32[1,1,6400]{2,1,0:T(1,128)} %param.9) | copy-start | bytes 76804
  21.0 17.3 %all-to-all-start = ((f32[16,1,1,3840]{3,2,1,0:T(1,128)}), f32[16,1,1,3840]{3,2,1,0:T(1,128)S(1)}, u32[]{:S(2)}, u32[]{:S(2)}) async-start(f32[16,1,1,3840]{3,2,1,0:T(1,128)} %constant_dynamic-update-slice_fusion), calls=%async_computation | async-start | bytes 491520 | tf_op jit(solution)/shard_map/all_to_all | solution.py:94
  39.4 28.7 %collective-permute-start.1 = (f32[15,4096]{1,0:T(8,128)S(1)}, f32[15,4096]{1,0:T(8,128)S(1)}, u32[]{:S(2)}, u32[]{:S(2)}) collective-permute-start(f32[15,4096]{1,0:T(8,128)S(1)} %bitcast.117), channel_id=1, source_target_pairs={{0,2},{2,4},{4,6},{6,8},{8,10},{10,12},{12,14},{14,16},{16,18},{18... | collective-permute-start | bytes 737288 | tf_op jit(solution)/shard_map/ppermute | solution.py:18
  41.5 26.6 %collective-permute-start = (f32[10,4096]{1,0:T(8,128)S(1)}, f32[10,4096]{1,0:T(8,128)S(1)}, u32[]{:S(2)}, u32[]{:S(2)}) collective-permute-start(f32[10,4096]{1,0:T(8,128)S(1)} %bitcast.123), channel_id=1, source_target_pairs={{0,4},{2,6},{4,8},{6,10},{8,12},{10,14},{12,16},{14,18},{16,20},{1... | collective-permute-start | bytes 491528 | tf_op jit(solution)/shard_map/ppermute | solution.py:18
  78.3 1.6 %copy-start = (f32[3,4096]{1,0:T(4,128)S(1)}, f32[3,4096]{1,0:T(4,128)}, u32[]{:S(2)}) copy-start(f32[3,4096]{1,0:T(4,128)} %get-tuple-element.128) | copy-start | bytes 147460
  82.3 19.9 %collective-permute-start.2 = (bf16[3,30,4096]{2,1,0:T(8,128)(2,1)S(1)}, bf16[3,30,4096]{2,1,0:T(8,128)(2,1)S(1)}, u32[]{:S(2)}, u32[]{:S(2)}) collective-permute-start(bf16[3,30,4096]{2,1,0:T(8,128)(2,1)S(1)} %multiply_convert_fusion), channel_id=1, source_target_pairs={{0,1},{1,0},{2,3},{3,2},{4,5},{5,4},{6,7},{7,6},{8,9},{9,8},{10,11... | collective-permute-start | bytes 2211848 | tf_op jit(solution)/shard_map/ppermute | solution.py:28
  120.7 32.1 %collective-permute-start.3 = (bf16[3,4096]{1,0:T(4,128)(2,1)S(1)}, bf16[3,4096]{1,0:T(4,128)(2,1)S(1)}, u32[]{:S(2)}, u32[]{:S(2)}) collective-permute-start(bf16[3,4096]{1,0:T(4,128)(2,1)S(1)} %convert_element_type.58), channel_id=1, source_target_pairs={{0,1},{1,0},{2,3},{3,2},{4,5},{5,4},{6,7},{7,6},{8,9},{9,8},{10,11... | collective-permute-start | bytes 73736 | tf_op jit(solution)/shard_map/ppermute | solution.py:28
